TPU v7x, 256 devices: a whole 4x4x8 slice. The times are simulated.
256 devices in a mesh: dp: 32 (over y_hi, z, core), vocab: 8 (over x, y_lo).
Axes of the slice: x: 4, y: 4 (y_hi: 2, y_lo: 2; y = y_hi * 2 + y_lo), z: 8, core: 2. Of those that a mesh axis runs over, the one named last changes fastest.
Arguments:
- hidden: bfloat16 [16384, 3072], P(('dp', 'vocab')), may hold values from -128 to 128
- targets: int32 [16384], P(('dp', 'vocab')), may hold values from 0 to 16383
- lengths: int32 [32], P('dp'), may hold values from 1 to 512
- head: bfloat16 [3072, 16384], P('dp', 'vocab'), may hold values from -1 to 1
Outputs:
- grad_hidden: bfloat16 [16384, 3072], P(('dp', 'vocab'))
- loss: float32 [], replicated
All inputs are finite; a program needn't handle non-finite values.
Results may differ from a plain program's by a relative error of at most 0.0052.
Values may be sent and summed in bfloat16 or wider, within the bound.
A program may use at most 64 MiB of HBM per device.

v0:
```python
import functools
import jax
import jax.numpy as jnp
from jax import lax
from jax.sharding import Mesh
from jax.sharding import PartitionSpec as P

DP = ("dp_0", "dp_1", "dp_2")
VOCAB = ("vocab_0", "vocab_1")
DP_VOCAB = ("dp_0", "dp_1", "dp_2", "vocab_0", "vocab_1")


def whole_of(shard, axes, dim):
    filled = shard
    for number in range(len(axes) - 1, -1, -1):
        filled = lax.all_gather(filled, axes[number], axis=dim, tiled=True)
    return filled


def all_in_one(shard, axis):
    leaves = jax.tree.leaves(shard)
    sequence = sorted(range(len(leaves)), key=lambda k: -leaves[k].size)
    width = (1, *leaves[sequence[0]].shape)[-1]
    lines = [
        jnp.pad(leaves[k].reshape(-1), (0, -leaves[k].size % width)).reshape(-1, width)
        for k in sequence
    ]
    both, at, found = (lax.all_gather(jnp.concatenate(lines), axis), 0, {})
    for k, line in zip(sequence, lines):
        share = both[:, at : at + len(line)].reshape(len(both), -1)
        found[k] = share[:, : leaves[k].size].reshape(-1, *leaves[k].shape)
        at += len(line)
    numbers = iter(range(len(leaves)))
    return jax.tree.map(lambda _: found[next(numbers)], shard)


def combined_all(shard, axis, combine):
    everything = all_in_one(shard, axis)
    first = jax.tree.map(lambda part: part[0], everything)

    def turn(k, so_far):
        return combine(so_far, jax.tree.map(lambda part: part[k], everything))

    return lax.fori_loop(1, lax.axis_size(axis), turn, first)


def one_axis_at_a_time(shard, axes):
    return functools.reduce(lax.psum, axes, shard)


def merge_rows(earlier, later):
    maxima = jnp.maximum(earlier[0], later[0])
    totals = earlier[1] * jnp.exp(earlier[0] - maxima) + later[1] * jnp.exp(later[0] - maxima)
    return (maxima, totals, earlier[2] + later[2])


def local(hidden, targets, lengths, head):
    whole_head, all_lengths = (
        lax.all_gather(head, DP, axis=0, tiled=True),
        lax.all_gather(lengths, DP, axis=0, tiled=True),
    )
    clip_rows, clip_targets = (whole_of(hidden, VOCAB, 0), whole_of(targets, VOCAB, 0))
    level_count = whole_head.shape[1]
    home_rows = hidden.shape[0]
    logits = jnp.dot(clip_rows, whole_head, preferred_element_type=jnp.float32)
    local_levels = clip_targets - lax.axis_index(VOCAB) * level_count
    level_grid = jnp.arange(level_count, dtype=jnp.int32)
    is_target = local_levels[:, None] == level_grid[None, :]
    target_logit = jnp.sum(jnp.where(is_target, logits, 0.0), axis=1)
    maxima = jnp.max(logits, axis=1)
    totals = jnp.sum(jnp.exp(logits - maxima[:, None]), axis=1)
    maxima, totals, target_logit = combined_all((maxima, totals, target_logit), VOCAB, merge_rows)
    log_total = maxima + jnp.log(totals)
    total_count = jnp.sum(all_lengths).astype(jnp.float32)
    clip_index = jnp.arange(all_lengths.shape[0], dtype=jnp.int32)
    clip_length = jnp.sum(jnp.where(clip_index == lax.axis_index(DP), all_lengths, 0))
    positions = jnp.arange(clip_rows.shape[0], dtype=jnp.int32)
    valid_rows = (positions < clip_length).astype(jnp.float32)
    row_loss = valid_rows * (log_total - target_logit)
    home_loss = jnp.sum(
        lax.dynamic_slice_in_dim(row_loss, lax.axis_index(VOCAB) * home_rows, home_rows, 0)
    )
    loss = one_axis_at_a_time(home_loss, DP_VOCAB) / total_count
    weights = (valid_rows / total_count)[:, None]
    grad_logits = (
        weights * (jnp.exp(logits - log_total[:, None]) - is_target.astype(jnp.float32))
    ).astype(jnp.bfloat16)
    grad_home = lax.psum_scatter(
        lax.dot_general(
            grad_logits, whole_head, (((1,), (1,)), ((), ())), preferred_element_type=jnp.float32
        ),
        VOCAB,
        scatter_dimension=0,
        tiled=True,
    )
    return (grad_home.astype(jnp.bfloat16), loss)


def solution(mesh):
    torus = Mesh(
        mesh.devices.reshape(2, 8, 2, 4, 2), ("dp_0", "dp_1", "dp_2", "vocab_0", "vocab_1")
    )
    return jax.shard_map(
        local,
        mesh=torus,
        in_specs=(P(DP_VOCAB, None), P(DP_VOCAB), P(DP), P(DP, VOCAB)),
        out_specs=(P(DP_VOCAB, None), P()),
        check_vma=False,
    )
```

profile of v0, /device:TPU:1, one launch (start us, length us, event | category | flops | bytes accessed | tf_op | source)
XLA Modules:
  0.0 381.4 jit_solution(14241844789752872180)
XLA Ops:
  7.2 13.1 %all_gather.25 = bf16[128,3072]{1,0:T(8,128)(2,1)} all-gather(bf16[64,3072]{1,0:T(8,128)(2,1)} %param.6), channel_id=1, replica_groups=mesh['dp_0'=2,'dp_1'=8,'dp_2'=2,'vocab_0'=4,'vocab_1'=2] {'vocab_1'}, dimensions={0}, use_global_device_ids=true | all-gather | bytes 1179648 | tf_op jit(solution)/shard_map/all_gather | solution.py:16
  20.4 0.7 all-gather.8.cloned.1.call-update
  21.8 1.3 dynamic-slice.1
  23.1 1.2 dynamic-slice
  24.3 0.7 dynamic-update-slice
  25.0 18.6 %all-reduce = s32[32]{0:T(128)S(1)} all-reduce(s32[32]{0:T(128)S(1)} %dynamic-update-slice), channel_id=1, replica_groups=mesh['dp_0'=2,'dp_1'=8,'dp_2'=2,'vocab_0'=4,'vocab_1'=2] {'dp_0','dp_1',..., use_global_device_ids=true, to_apply=%add | all-reduce | flops 32 | bytes 256
  45.6 0.9 dynamic-update-slice.1
  46.4 3.5 all-reduce.1
  49.9 8.8 %all-gather.1 = s32[4,1,128]{2,1,0:T(1,128)S(1)} all-gather(s32[1,1,128]{2,1,0:T(1,128)S(1)} %bitcast.43), channel_id=1, replica_groups=mesh['dp_0'=2,'dp_1'=8,'dp_2'=2,'vocab_0'=4,'vocab_1'=2] {'vocab_0'}, dimensions={0}, use_global_device_ids=true | all-gather | bytes 2560 | tf_op jit(solution)/shard_map/all_gather | solution.py:16
  59.3 6.9 %all-gather.6.cloned.1.call-done = bf16[512,3072]{1,0:T(8,128)(2,1)} async-done(((bf16[128,3072]{1,0:T(8,128)(2,1)}), bf16[512,3072]{1,0:T(8,128)(2,1)}) %all-gather.6.cloned.1.call-update) | async-done | bytes 3145744 | tf_op jit(solution)/shard_map/all_gather | solution.py:16
  66.1 120.7 %all-gather.8.cloned.1.call-done = bf16[3072,2048]{1,0:T(8,128)(2,1)} async-done(((bf16[96,2048]{1,0:T(8,128)(2,1)}), bf16[3072,2048]{1,0:T(8,128)(2,1)}) %all-gather.8.cloned.1.call-update) | async-done | bytes 12582928 | tf_op jit(solution)/shard_map/all_gather | solution.py:59
  186.8 10.7 %fusion.8 = (f32[512]{0:T(512)S(1)}, f32[512,2048]{1,0:T(8,128)S(1)}) fusion(bf16[512,3072]{1,0:T(8,128)(2,1)} %all-gather.6.cloned.1.call-done, bf16[3072,2048]{1,0:T(8,128)(2,1)} %all-gather.8.cloned.1.call-done), kind=kOutput, calls=%fused_computation.26 | convolution fusion | flops 6443499008 | bytes 19924992 | tf_op jit(solution)/shard_map/dot_general | solution.py:65
  197.5 2.0 copy-done
  199.6 1.1 exponential_reduce_fusion
  200.7 21.8 %all-gather.2 = f32[8,3,512]{2,1,0:T(4,128)S(1)} all-gather(f32[1,3,512]{2,1,0:T(4,128)S(1)} %maximum_bitcast_fusion), channel_id=2, replica_groups=mesh['dp_0'=2,'dp_1'=8,'dp_2'=2,'vocab_0'=4,'vocab_1'=2] {'vocab_0','voc..., dimensions={0}, use_global_device_ids=true | all-gather | bytes 55296 | tf_op jit(solution)/shard_map/all_gather | solution.py:28
  223.8 13.1 %fusion = f32[512,3072]{1,0:T(8,128)} fusion(bf16[3072,2048]{1,0:T(8,128)(2,1)} %all-gather.8.cloned.1.call-done, f32[512,2048]{1,0:T(8,128)} %copy-done, f32[512]{0:T(512)S(1)} %get-tuple-element.204, s32[512]{0:T(512)S(1)} %bitcast.42, f32[512]{0:T(512)S(1)} %fusion.4), kind=kOutput, calls=%fused_computation.8 | convolution fusion | flops 6448742400 | bytes 23074816 | tf_op jit(solution)/shard_map/dot_general | solution.py:89
  236.9 0.7 dynamic-slice_reduce_fusion
  237.6 5.9 %psum.35 = f32[]{:T(128)} all-reduce(f32[]{:T(128)} %dynamic-slice_reduce_fusion), channel_id=1, replica_groups=mesh['dp_0'=2,'dp_1'=8,'dp_2'=2,'vocab_0'=4,'vocab_1'=2] {'dp_0'}, use_global_device_ids=true, to_apply=%region_9.10 | all-reduce | flops 1 | bytes 8 | tf_op jit(solution)/shard_map/psum | solution.py:48
  243.5 13.3 %psum.36 = f32[]{:T(128)} all-reduce(f32[]{:T(128)} %psum.35), channel_id=1, replica_groups=mesh['dp_0'=2,'dp_1'=8,'dp_2'=2,'vocab_0'=4,'vocab_1'=2] {'dp_1'}, use_global_device_ids=true, to_apply=%region_10.11 | all-reduce | flops 1 | bytes 8 | tf_op jit(solution)/shard_map/psum | solution.py:48
  256.8 13.9 %psum.37 = f32[]{:T(128)} all-reduce(f32[]{:T(128)} %psum.36), channel_id=1, replica_groups=mesh['dp_0'=2,'dp_1'=8,'dp_2'=2,'vocab_0'=4,'vocab_1'=2] {'dp_2'}, use_global_device_ids=true, to_apply=%region_11.12 | all-reduce | flops 1 | bytes 8 | tf_op jit(solution)/shard_map/psum | solution.py:48
  270.7 6.9 %psum.38 = f32[]{:T(128)} all-reduce(f32[]{:T(128)} %psum.37), channel_id=1, replica_groups=mesh['dp_0'=2,'dp_1'=8,'dp_2'=2,'vocab_0'=4,'vocab_1'=2] {'vocab_0'}, use_global_device_ids=true, to_apply=%region_12.13 | all-reduce | flops 1 | bytes 8 | tf_op jit(solution)/shard_map/psum | solution.py:48
  277.5 6.2 %psum.39 = f32[]{:T(128)} all-reduce(f32[]{:T(128)} %psum.38), channel_id=1, replica_groups=mesh['dp_0'=2,'dp_1'=8,'dp_2'=2,'vocab_0'=4,'vocab_1'=2] {'vocab_1'}, use_global_device_ids=true, to_apply=%region_13.14 | all-reduce | flops 1 | bytes 8 | tf_op jit(solution)/shard_map/psum | solution.py:48
  284.4 87.4 %reduce-scatter.2.cloned.1.call-done = f32[64,3072]{1,0:T(8,128)} async-done(((f32[512,3072]{1,0:T(8,128)}), f32[64,3072]{1,0:T(8,128)}) %reduce-scatter.2.cloned.1.call-update) | async-done | bytes 786448 | tf_op jit(solution)/shard_map/reduce_scatter | solution.py:88
  371.8 1.9 convert_element_type.17
  (46 shorter events, 3.0 us)
Async XLA Ops:
  7.2 59.0 %all-gather.6.cloned.1.call-start = ((), (), s32[]{:S(2)}) async-start(), calls=%async_computation.1 | async-start | bytes 3932160 | tf_op jit(solution)/shard_map/all_gather | solution.py:16
  20.4 166.4 %all-gather.8.cloned.1.call-start = ((), (), s32[]{:S(2)}) async-start(), calls=%async_computation.2 | async-start | bytes 12976128 | tf_op jit(solution)/shard_map/all_gather | solution.py:59
  21.1 350.7 %reduce-scatter.2.cloned.1.call-start = ((), (), s32[]{:S(2)}) async-start(), calls=%async_computation.3 | async-start | bytes 7077888 | tf_op jit(solution)/shard_map/reduce_scatter | solution.py:88
  197.5 2.0 copy-start
Sparse Core Ops, SparseCore 0:
  20.5 45.5 all-gather.5
  68.9 117.8 all-gather.7
  237.0 134.7 reduce-scatter.1
where the time goes:
time: 382 us; the launch traced here: 381 us
  waiting for transfers between devices  216 us (57%)
  blocking collectives  112 us (29%)
  matrix products  23.8 us (6%)
  between operations  17.6 us (5%)
  local copies, waits for them, and re-layouts  6.23 us (2%)
  other arithmetic  5.71 us (1%)
    all_gather x1, waiting for transfers between devices, local(): lax.all_gather(head, DP, axis=0, tiled=True)  121 us
    reduce_scatter x1, waiting for transfers between devices, local(): lax.psum_scatter(lax.dot_general(grad_logits, whole_head, (((1,), (1,)),...  87.4 us
    psum x5, blocking collectives, one_axis_at_a_time(): return functools.reduce(lax.psum, axes, shard)  46.2 us
    unnamed x2, blocking collectives  22.1 us
    all_gather x2, blocking collectives, whole_of(): filled = lax.all_gather(filled, axes[number], axis=dim, tiled=True)  21.9 us
    all_gather x1, blocking collectives, all_in_one(): both, at, found = (lax.all_gather(jnp.concatenate(lines), axis), 0, {})  21.8 us
    dot_general x1, matrix products, local(): lax.dot_general(grad_logits, whole_head, (((1,), (1,)), ((), ())), prefer...  13.1 us
    dot_general x1, matrix products, local(): logits = jnp.dot(clip_rows, whole_head, preferred_element_type=jnp.float32)  10.7 us
  transfers between devices with their start and end apart: 3, of which 3 were waited for; matrix products, arithmetic and copies ran while one was open for 2% of the time, Pallas kernels for 0%

commit v1 on v0

--- a/solution.py
+++ b/solution.py
@@ -8,6 +8,21 @@
 DP = ("dp_0", "dp_1", "dp_2")
 VOCAB = ("vocab_0", "vocab_1")
 DP_VOCAB = ("dp_0", "dp_1", "dp_2", "vocab_0", "vocab_1")
+
+
+def _guide_ports(inputs, group_axis):
+    return jnp.concatenate(
+        lax.all_to_all(
+            jnp.stack(lax.axis_size(group_axis) * [inputs], axis=0),
+            group_axis,
+            split_axis=0,
+            concat_axis=0,
+        ),
+        axis=0,
+    )
+
+
+serve_roads = functools.partial(_guide_ports, group_axis=DP)
 
 
 def whole_of(shard, axes, dim):
@@ -55,10 +70,7 @@
 
 
 def local(hidden, targets, lengths, head):
-    whole_head, all_lengths = (
-        lax.all_gather(head, DP, axis=0, tiled=True),
-        lax.all_gather(lengths, DP, axis=0, tiled=True),
-    )
+    whole_head, all_lengths = (serve_roads(head), lax.all_gather(lengths, DP, axis=0, tiled=True))
     clip_rows, clip_targets = (whole_of(hidden, VOCAB, 0), whole_of(targets, VOCAB, 0))
     level_count = whole_head.shape[1]
     home_rows = hidden.shape[0]

time: 382 us -> 526 us (1.38)
  blocking collectives: 112 us -> 366 us
  waiting for transfers between devices: 216 us -> 86.4 us
  starting transfers between devices: 0.12 us -> 13 us
  local copies, waits for them, and re-layouts: 6.23 us -> 11.6 us
    unnamed x2, blocking collectives: 22.1 us -> 246 us
    all_gather x1 -> x0, waiting for transfers between devices: 121 us -> none  [local(): lax.all_gather(head, DP, axis=0, tiled=True)]
    all_gather x2, blocking collectives: 21.9 us -> 49.1 us  [whole_of(): filled = lax.all_gather(filled, axes[number], axis=dim, tiled=True)]
    all_to_all x0 -> x1, starting transfers between devices: none -> 12.9 us  [_guide_ports(): lax.all_to_all(jnp.stack(lax.axis_size(group_axis) * [inputs], axis=0), g...]
    another operation x0 -> x1, local copies, waits for them, and re-layouts: none -> 7.07 us  [_guide_ports(): jnp.stack(lax.axis_size(group_axis) * [inputs], axis=0)]
    all_gather x1, waiting for transfers between devices: 6.85 us -> 0.02 us  [whole_of(): filled = lax.all_gather(filled, axes[number], axis=dim, tiled=True)]
  transfers between devices with their start and end apart: 3 -> 3, of which waited for: 3 -> 1; matrix products, arithmetic and copies ran while one was open for 2% -> 1% of each run, Pallas kernels for 0% -> 0%
where the time goes in v1:
time: 526 us; the launch traced here: 525 us
  blocking collectives  366 us (70%)
  waiting for transfers between devices  86.4 us (16%)
  matrix products  23.8 us (5%)
  between operations  18 us (3%)
  starting transfers between devices  13 us (2%)
  local copies, waits for them, and re-layouts  11.6 us (2%)
  other arithmetic  6.01 us (1%)
    unnamed x2, blocking collectives  246 us
    reduce_scatter x1, waiting for transfers between devices, local(): lax.psum_scatter(lax.dot_general(grad_logits, whole_head, (((1,), (1,)),...  86.4 us
    psum x5, blocking collectives, one_axis_at_a_time(): return functools.reduce(lax.psum, axes, shard)  49.8 us
    all_gather x2, blocking collectives, whole_of(): filled = lax.all_gather(filled, axes[number], axis=dim, tiled=True)  49.1 us
    all_gather x1, blocking collectives, all_in_one(): both, at, found = (lax.all_gather(jnp.concatenate(lines), axis), 0, {})  21.9 us
    dot_general x1, matrix products, local(): lax.dot_general(grad_logits, whole_head, (((1,), (1,)), ((), ())), prefer...  13.1 us
    all_to_all x1, starting transfers between devices, _guide_ports(): lax.all_to_all(jnp.stack(lax.axis_size(group_axis) * [inputs], axis=0), g...  12.9 us
    dot_general x1, matrix products, local(): logits = jnp.dot(clip_rows, whole_head, preferred_element_type=jnp.float32)  10.7 us
  transfers between devices with their start and end apart: 3, of which 1 were waited for; matrix products, arithmetic and copies ran while one was open for 1% of the time, Pallas kernels for 0%

profile of v1, /device:TPU:1, one launch (start us, length us, event | category | flops | bytes accessed | tf_op | source)
XLA Modules:
  0.0 525.4 jit_solution(14798573958116979966)
XLA Ops:
  7.2 7.1 %stack.2 = bf16[32,96,2048]{2,1,0:T(8,128)(2,1)} broadcast(bf16[96,2048]{1,0:T(8,128)(2,1)} %param.9), dimensions={1,2} | broadcast | bytes 12976128 | tf_op jit(solution)/shard_map/stack | solution.py:16
  14.2 12.9 %all-to-all-start = ((bf16[32,96,2048]{2,1,0:T(8,128)(2,1)}), bf16[32,96,2048]{2,1,0:T(8,128)(2,1)}, u32[]{:S(2)}, u32[]{:S(2)}) async-start(bf16[32,96,2048]{2,1,0:T(8,128)(2,1)} %stack.2), calls=%async_computation | async-start | bytes 25165824 | tf_op jit(solution)/shard_map/all_to_all | solution.py:15
  27.2 41.4 %all_gather.22 = bf16[128,3072]{1,0:T(8,128)(2,1)} all-gather(bf16[64,3072]{1,0:T(8,128)(2,1)S(1)} %copy-done.1), channel_id=1, replica_groups=mesh['dp_0'=2,'dp_1'=8,'dp_2'=2,'vocab_0'=4,'vocab_1'=2] {'vocab_1'}, dimensions={0}, use_global_device_ids=true | all-gather | bytes 1179648 | tf_op jit(solution)/shard_map/all_gather | solution.py:31
  69.9 0.6 dynamic-slice
  70.6 0.8 dynamic-update-slice
  71.4 242.5 %all-reduce = s32[32]{0:T(128)S(1)} all-reduce(s32[32]{0:T(128)S(1)} %dynamic-update-slice), channel_id=1, replica_groups=mesh['dp_0'=2,'dp_1'=8,'dp_2'=2,'vocab_0'=4,'vocab_1'=2] {'dp_0','dp_1',..., use_global_device_ids=true, to_apply=%add | all-reduce | flops 32 | bytes 256
  313.9 0.7 fusion.5
  316.2 3.1 all-reduce.1
  319.3 7.7 %all-gather.1 = s32[4,1,128]{2,1,0:T(1,128)S(1)} all-gather(s32[1,1,128]{2,1,0:T(1,128)S(1)} %bitcast.44), channel_id=1, replica_groups=mesh['dp_0'=2,'dp_1'=8,'dp_2'=2,'vocab_0'=4,'vocab_1'=2] {'vocab_0'}, dimensions={0}, use_global_device_ids=true | all-gather | bytes 2560 | tf_op jit(solution)/shard_map/all_gather | solution.py:31
  327.0 0.7 fusion.4
  327.7 10.7 %fusion.8 = (f32[512]{0:T(512)S(1)}, f32[512,2048]{1,0:T(8,128)S(1)}) fusion(bf16[512,3072]{1,0:T(8,128)(2,1)} %all-gather.5.cloned.1.call-done, bf16[3072,2048]{1,0:T(8,128)(2,1)} %bitcast.4), kind=kOutput, calls=%fused_computation.26 | convolution fusion | flops 6443499008 | bytes 19924992 | tf_op jit(solution)/shard_map/dot_general | solution.py:77
  338.4 2.0 copy-done
  340.5 1.1 exponential_reduce_fusion
  341.6 21.9 %all-gather.2 = f32[8,3,512]{2,1,0:T(4,128)S(1)} all-gather(f32[1,3,512]{2,1,0:T(4,128)S(1)} %maximum_bitcast_fusion), channel_id=2, replica_groups=mesh['dp_0'=2,'dp_1'=8,'dp_2'=2,'vocab_0'=4,'vocab_1'=2] {'vocab_0','voc..., dimensions={0}, use_global_device_ids=true | all-gather | bytes 55296 | tf_op jit(solution)/shard_map/all_gather | solution.py:43
  364.2 0.7 subtract_select_fusion
  364.9 13.1 %fusion = f32[512,3072]{1,0:T(8,128)} fusion(bf16[3072,2048]{1,0:T(8,128)(2,1)} %bitcast.4, f32[512,2048]{1,0:T(8,128)} %copy-done, f32[512]{0:T(512)S(1)} %get-tuple-element.204, s32[512]{0:T(512)S(1)} %bitcast.43, f32[512]{0:T(512)S(1)} %fusion.4), kind=kOutput, calls=%fused_computation.8 | convolution fusion | flops 6448742400 | bytes 23074816 | tf_op jit(solution)/shard_map/dot_general | solution.py:101
  378.0 0.7 dynamic-slice_reduce_fusion
  378.6 5.9 %psum.35 = f32[]{:T(128)} all-reduce(f32[]{:T(128)} %dynamic-slice_reduce_fusion), channel_id=1, replica_groups=mesh['dp_0'=2,'dp_1'=8,'dp_2'=2,'vocab_0'=4,'vocab_1'=2] {'dp_0'}, use_global_device_ids=true, to_apply=%region_9.10 | all-reduce | flops 1 | bytes 8 | tf_op jit(solution)/shard_map/psum | solution.py:63
  384.5 11.3 %psum.36 = f32[]{:T(128)} all-reduce(f32[]{:T(128)} %psum.35), channel_id=1, replica_groups=mesh['dp_0'=2,'dp_1'=8,'dp_2'=2,'vocab_0'=4,'vocab_1'=2] {'dp_1'}, use_global_device_ids=true, to_apply=%region_10.11 | all-reduce | flops 1 | bytes 8 | tf_op jit(solution)/shard_map/psum | solution.py:63
  395.8 20.1 %psum.37 = f32[]{:T(128)} all-reduce(f32[]{:T(128)} %psum.36), channel_id=1, replica_groups=mesh['dp_0'=2,'dp_1'=8,'dp_2'=2,'vocab_0'=4,'vocab_1'=2] {'dp_2'}, use_global_device_ids=true, to_apply=%region_11.12 | all-reduce | flops 1 | bytes 8 | tf_op jit(solution)/shard_map/psum | solution.py:63
  416.0 7.5 %psum.38 = f32[]{:T(128)} all-reduce(f32[]{:T(128)} %psum.37), channel_id=1, replica_groups=mesh['dp_0'=2,'dp_1'=8,'dp_2'=2,'vocab_0'=4,'vocab_1'=2] {'vocab_0'}, use_global_device_ids=true, to_apply=%region_12.13 | all-reduce | flops 1 | bytes 8 | tf_op jit(solution)/shard_map/psum | solution.py:63
  423.5 5.0 psum.39
  429.1 86.4 %reduce-scatter.2.cloned.1.call-done = f32[64,3072]{1,0:T(8,128)} async-done(((f32[512,3072]{1,0:T(8,128)}), f32[64,3072]{1,0:T(8,128)}) %reduce-scatter.2.cloned.1.call-update) | async-done | bytes 786448 | tf_op jit(solution)/shard_map/reduce_scatter | solution.py:100
  515.5 1.9 convert_element_type.17
  (54 shorter events, 2.0 us)
Async XLA Ops:
  14.2 13.0 %copy-start.1 = (bf16[64,3072]{1,0:T(8,128)(2,1)S(1)}, bf16[64,3072]{1,0:T(8,128)(2,1)}, u32[]{:S(2)}) copy-start(bf16[64,3072]{1,0:T(8,128)(2,1)} %param.6) | copy-start | bytes 1179652
  14.2 55.1 %copy-start.4 = (u32[256]{0:T(256)S(1)}, u32[256]{0:T(256)}, u32[]{:S(2)}) copy-start(u32[256]{0:T(256)} %constant.85) | copy-start | bytes 3076
  14.2 55.7 %copy-start.3 = (u32[256]{0:T(256)S(1)}, u32[256]{0:T(256)}, u32[]{:S(2)}) copy-start(u32[256]{0:T(256)} %constant.80) | copy-start | bytes 3076
  14.2 301.7 %copy-start.2 = (s32[64]{0:T(128)S(1)}, s32[64]{0:T(128)}, u32[]{:S(2)}) copy-start(s32[64]{0:T(128)} %param.7) | copy-start | bytes 772
  14.2 313.4 %all-to-all-start = ((bf16[32,96,2048]{2,1,0:T(8,128)(2,1)}), bf16[32,96,2048]{2,1,0:T(8,128)(2,1)}, u32[]{:S(2)}, u32[]{:S(2)}) async-start(bf16[32,96,2048]{2,1,0:T(8,128)(2,1)} %stack.2), calls=%async_computation | async-start | bytes 25165824 | tf_op jit(solution)/shard_map/all_to_all | solution.py:15
  27.2 300.5 %all-gather.5.cloned.1.call-start = ((), (), s32[]{:S(2)}) async-start(), calls=%async_computation.2 | async-start | bytes 3932160 | tf_op jit(solution)/shard_map/all_gather | solution.py:31
  68.6 446.9 %reduce-scatter.2.cloned.1.call-start = ((), (), s32[]{:S(2)}) async-start(), calls=%async_computation.3 | async-start | bytes 7077888 | tf_op jit(solution)/shard_map/reduce_scatter | solution.py:100
  338.4 2.0 copy-start
Sparse Core Ops, SparseCore 0:
  68.8 45.8 all-gather.4
  378.1 137.3 reduce-scatter.1
